TPU v7x, 32 devices: a whole 2x2x4 slice. The times are simulated.
32 devices in a mesh: parts: 2 (over y), blk: 4 (over z), sub: 2 (over x), rep: 2 (over core).
Axes of the slice: x: 2, y: 2, z: 4, core: 2. Of those that a mesh axis runs over, the one named last changes fastest.
Arguments:
- queries: bfloat16 [128, 32, 128], P(('parts', 'blk', 'sub', 'rep')), parts along dimension 0, may hold values from -1.5 to 1.5
- passages: bfloat16 [512, 128, 128], P(('parts', 'blk')), parts along dimension 0, may hold values from -1.5 to 1.5
- lengths: int32 [512], P(('parts', 'blk')), parts along dimension 0, may hold values from 8 to 128
- slot_of: int32 [512], P('parts'), parts along dimension 0, may hold values from 0 to 255, each once
- candidates: int32 [128, 256], P(('parts', 'blk', 'sub', 'rep')), parts along dimension 0, may hold values from 0 to 255
Outputs:
- score: float32 [128, 256], P(('parts', 'blk', 'sub', 'rep')), parts along dimension 0
- top: float32 [128, 10], P(('parts', 'blk', 'sub', 'rep')), parts along dimension 0
There are 2 independent parts, one for each index of `parts`. A program takes and returns all parts, laid end to end along the dimension named above; each array names one. Nothing has to cross between parts.
Inputs may be any that keep to these rules, and one draw needn't show every extreme that they name: `slot_of`: a permutation; storage row r lies on the blk index r // 64. `candidates`: passage ids, repeats allowed. `lengths`: the live slots of a row are its first ones.
All inputs are finite; a program needn't handle non-finite values.
Results may differ from a plain program's by a relative error of at most 0.0003.
Values may be sent and summed in bfloat16 or wider, within the bound.
A program may use at most 64 MiB of HBM per device.

v0:
```python
import jax
import jax.numpy as jnp
from jax import lax
from jax.sharding import PartitionSpec as P

TOPN = 10


def score_table(rows_q, passages, lengths):
    queries_here = rows_q.shape[0]
    tokens = rows_q.shape[1]
    width = rows_q.shape[2]
    count = passages.shape[0]
    span = passages.shape[1]
    group = 4
    flat = rows_q.reshape(queries_here * tokens, width)
    blocks = passages.reshape(count // group, group * span, width)
    spans = lengths.reshape(count // group, group)

    def one_block(pair):
        piece, live_count = pair
        similar = lax.dot_general(
            flat, piece, (((1,), (1,)), ((), ())), preferred_element_type=jnp.float32
        )
        similar = similar.reshape(queries_here * tokens, group, span)
        live = lax.broadcasted_iota(jnp.int32, (group, span), 1) < live_count[:, None]
        best = jnp.max(jnp.where(live[None], similar, -1e30), axis=2)
        return jnp.sum(best.reshape(queries_here, tokens, group), axis=1) / tokens

    table = lax.map(one_block, (blocks, spans))
    return jnp.transpose(table, (1, 0, 2)).reshape(queries_here, count)


def shards(queries, passages, lengths, slot_of, candidates):
    table = score_table(lax.all_gather(queries, "blk", axis=0, tiled=True), passages, lengths)
    whole = lax.all_to_all(table, "blk", split_axis=0, concat_axis=1, tiled=True)
    score = jnp.take_along_axis(whole, jnp.take(slot_of, candidates, axis=0), axis=1)
    top = lax.top_k(score, TOPN)[0]
    return (score, top)


def solution(mesh):
    return jax.shard_map(
        shards,
        mesh=mesh,
        in_specs=(
            P(("parts", "blk", "sub", "rep"), None, None),
            P(("parts", "blk"), None, None),
            P(("parts", "blk")),
            P("parts"),
            P(("parts", "blk", "sub", "rep"), None),
        ),
        out_specs=(
            P(("parts", "blk", "sub", "rep"), None),
            P(("parts", "blk", "sub", "rep"), None),
        ),
        check_vma=False,
    )
```

profile of v0, /device:TPU:0, one launch (start us, length us, event | category | flops | bytes accessed | tf_op | source)
XLA Modules:
  0.0 66.2 jit_solution(11829611261535838261)
XLA Ops:
  0.7 0.7 %reshape.67 = s32[16,4]{1,0:T(8,128)S(1)} reshape(s32[64]{0:T(128)} %param.9) | data formatting | bytes 512 | tf_op jit(solution)/shard_map/reshape | solution.py:18
  1.4 15.3 %all_gather.3 = bf16[16,32,128]{2,1,0:T(8,128)(2,1)S(1)} all-gather(bf16[4,32,128]{2,1,0:T(8,128)(2,1)} %param.7), channel_id=1, replica_groups=mesh['parts'=2,'blk'=4,'sub'=2,'rep'=2] {'blk'}, dimensions={0}, use_global_device_ids=true | all-gather | bytes 163840 | tf_op jit(solution)/shard_map/all_gather | solution.py:35
  16.7 24.2 %while.10 = (s32[]{:T(128)}, f32[16,16,4]{1,2,0:T(4,128)S(1)}, s32[16,4]{1,0:T(8,128)S(1)}, bf16[16,512,128]{2,1,0:T(8,128)(2,1)}, bf16[512,128]{1,0:T(8,128)(2,1)S(1)}, /*index=5*/s32[]{:T(128)}, f32[]{:T(128)}) while((s32[]{:T(128)}, f32[16,16,4]{1,2,0:T(4,128)S(1)}, s32[16,4]{1,0:T(8,128)S(1)}, bf16[16,512,128]{2,1,0:T(8,128)(2,1)}, ...), condition=%wide.region_3.4_spmd, body=%wide.region_0.3_spmd.sunk | while | flops 67633664 | bytes 300437 | solution.py:30
  16.8 1.2 %select_reduce_fusion.2 = f32[512,4]{0,1:T(4,128)S(1)} fusion(pred[4,128]{1,0:T(4,128)(4,1)S(1)} %iota_compare_fusion.2, bf16[512,128]{1,0:T(8,128)(2,1)S(1)} %get-tuple-element.93, bf16[16,512,128]{2,1,0:T(8,128)(2,1)} %get-tuple-element.92, s32[]{:T(128)S(6)} %copy.17), kind=kOutput, calls=%fused_computation.2.clone.1 | convolution fusion | flops 67631104 | bytes 270852 | tf_op jit(solution)/shard_map/while/body/eval_jaxpr/dot_general | solution.py:22
  18.0 0.1 reshape.95
  18.1 0.1 reduce_sum.10
  18.3 1.2 %select_reduce_fusion.2 = f32[512,4]{0,1:T(4,128)S(1)} fusion(pred[4,128]{1,0:T(4,128)(4,1)S(1)} %iota_compare_fusion.2, bf16[512,128]{1,0:T(8,128)(2,1)S(1)} %get-tuple-element.93, bf16[16,512,128]{2,1,0:T(8,128)(2,1)} %get-tuple-element.92, s32[]{:T(128)S(6)} %copy.17), kind=kOutput, calls=%fused_computation.2.clone.1 | convolution fusion | flops 67631104 | bytes 270852 | tf_op jit(solution)/shard_map/while/body/eval_jaxpr/dot_general | solution.py:22
  19.5 0.1 reshape.95
  19.6 0.1 reduce_sum.10
  19.8 1.2 %select_reduce_fusion.2 = f32[512,4]{0,1:T(4,128)S(1)} fusion(pred[4,128]{1,0:T(4,128)(4,1)S(1)} %iota_compare_fusion.2, bf16[512,128]{1,0:T(8,128)(2,1)S(1)} %get-tuple-element.93, bf16[16,512,128]{2,1,0:T(8,128)(2,1)} %get-tuple-element.92, s32[]{:T(128)S(6)} %copy.17), kind=kOutput, calls=%fused_computation.2.clone.1 | convolution fusion | flops 67631104 | bytes 270852 | tf_op jit(solution)/shard_map/while/body/eval_jaxpr/dot_general | solution.py:22
  21.1 0.1 reduce_sum.10
  21.3 1.2 %select_reduce_fusion.2 = f32[512,4]{0,1:T(4,128)S(1)} fusion(pred[4,128]{1,0:T(4,128)(4,1)S(1)} %iota_compare_fusion.2, bf16[512,128]{1,0:T(8,128)(2,1)S(1)} %get-tuple-element.93, bf16[16,512,128]{2,1,0:T(8,128)(2,1)} %get-tuple-element.92, s32[]{:T(128)S(6)} %copy.17), kind=kOutput, calls=%fused_computation.2.clone.1 | convolution fusion | flops 67631104 | bytes 270852 | tf_op jit(solution)/shard_map/while/body/eval_jaxpr/dot_general | solution.py:22
  22.6 0.1 reduce_sum.10
  22.8 1.2 %select_reduce_fusion.2 = f32[512,4]{0,1:T(4,128)S(1)} fusion(pred[4,128]{1,0:T(4,128)(4,1)S(1)} %iota_compare_fusion.2, bf16[512,128]{1,0:T(8,128)(2,1)S(1)} %get-tuple-element.93, bf16[16,512,128]{2,1,0:T(8,128)(2,1)} %get-tuple-element.92, s32[]{:T(128)S(6)} %copy.17), kind=kOutput, calls=%fused_computation.2.clone.1 | convolution fusion | flops 67631104 | bytes 270852 | tf_op jit(solution)/shard_map/while/body/eval_jaxpr/dot_general | solution.py:22
  24.2 0.1 reduce_sum.10
  24.4 1.2 %select_reduce_fusion.2 = f32[512,4]{0,1:T(4,128)S(1)} fusion(pred[4,128]{1,0:T(4,128)(4,1)S(1)} %iota_compare_fusion.2, bf16[512,128]{1,0:T(8,128)(2,1)S(1)} %get-tuple-element.93, bf16[16,512,128]{2,1,0:T(8,128)(2,1)} %get-tuple-element.92, s32[]{:T(128)S(6)} %copy.17), kind=kOutput, calls=%fused_computation.2.clone.1 | convolution fusion | flops 67631104 | bytes 270852 | tf_op jit(solution)/shard_map/while/body/eval_jaxpr/dot_general | solution.py:22
  25.7 0.1 reduce_sum.10
  25.9 1.2 %select_reduce_fusion.2 = f32[512,4]{0,1:T(4,128)S(1)} fusion(pred[4,128]{1,0:T(4,128)(4,1)S(1)} %iota_compare_fusion.2, bf16[512,128]{1,0:T(8,128)(2,1)S(1)} %get-tuple-element.93, bf16[16,512,128]{2,1,0:T(8,128)(2,1)} %get-tuple-element.92, s32[]{:T(128)S(6)} %copy.17), kind=kOutput, calls=%fused_computation.2.clone.1 | convolution fusion | flops 67631104 | bytes 270852 | tf_op jit(solution)/shard_map/while/body/eval_jaxpr/dot_general | solution.py:22
  27.2 0.1 reduce_sum.10
  27.4 1.2 %select_reduce_fusion.2 = f32[512,4]{0,1:T(4,128)S(1)} fusion(pred[4,128]{1,0:T(4,128)(4,1)S(1)} %iota_compare_fusion.2, bf16[512,128]{1,0:T(8,128)(2,1)S(1)} %get-tuple-element.93, bf16[16,512,128]{2,1,0:T(8,128)(2,1)} %get-tuple-element.92, s32[]{:T(128)S(6)} %copy.17), kind=kOutput, calls=%fused_computation.2.clone.1 | convolution fusion | flops 67631104 | bytes 270852 | tf_op jit(solution)/shard_map/while/body/eval_jaxpr/dot_general | solution.py:22
  28.7 0.1 reduce_sum.10
  28.9 1.2 %select_reduce_fusion.2 = f32[512,4]{0,1:T(4,128)S(1)} fusion(pred[4,128]{1,0:T(4,128)(4,1)S(1)} %iota_compare_fusion.2, bf16[512,128]{1,0:T(8,128)(2,1)S(1)} %get-tuple-element.93, bf16[16,512,128]{2,1,0:T(8,128)(2,1)} %get-tuple-element.92, s32[]{:T(128)S(6)} %copy.17), kind=kOutput, calls=%fused_computation.2.clone.1 | convolution fusion | flops 67631104 | bytes 270852 | tf_op jit(solution)/shard_map/while/body/eval_jaxpr/dot_general | solution.py:22
  30.2 0.1 reduce_sum.10
  30.4 1.2 %select_reduce_fusion.2 = f32[512,4]{0,1:T(4,128)S(1)} fusion(pred[4,128]{1,0:T(4,128)(4,1)S(1)} %iota_compare_fusion.2, bf16[512,128]{1,0:T(8,128)(2,1)S(1)} %get-tuple-element.93, bf16[16,512,128]{2,1,0:T(8,128)(2,1)} %get-tuple-element.92, s32[]{:T(128)S(6)} %copy.17), kind=kOutput, calls=%fused_computation.2.clone.1 | convolution fusion | flops 67631104 | bytes 270852 | tf_op jit(solution)/shard_map/while/body/eval_jaxpr/dot_general | solution.py:22
  31.7 0.1 reduce_sum.10
  31.9 1.2 %select_reduce_fusion.2 = f32[512,4]{0,1:T(4,128)S(1)} fusion(pred[4,128]{1,0:T(4,128)(4,1)S(1)} %iota_compare_fusion.2, bf16[512,128]{1,0:T(8,128)(2,1)S(1)} %get-tuple-element.93, bf16[16,512,128]{2,1,0:T(8,128)(2,1)} %get-tuple-element.92, s32[]{:T(128)S(6)} %copy.17), kind=kOutput, calls=%fused_computation.2.clone.1 | convolution fusion | flops 67631104 | bytes 270852 | tf_op jit(solution)/shard_map/while/body/eval_jaxpr/dot_general | solution.py:22
  33.2 0.1 reduce_sum.10
  33.5 1.2 %select_reduce_fusion.2 = f32[512,4]{0,1:T(4,128)S(1)} fusion(pred[4,128]{1,0:T(4,128)(4,1)S(1)} %iota_compare_fusion.2, bf16[512,128]{1,0:T(8,128)(2,1)S(1)} %get-tuple-element.93, bf16[16,512,128]{2,1,0:T(8,128)(2,1)} %get-tuple-element.92, s32[]{:T(128)S(6)} %copy.17), kind=kOutput, calls=%fused_computation.2.clone.1 | convolution fusion | flops 67631104 | bytes 270852 | tf_op jit(solution)/shard_map/while/body/eval_jaxpr/dot_general | solution.py:22
  34.8 0.1 reduce_sum.10
  35.0 1.2 %select_reduce_fusion.2 = f32[512,4]{0,1:T(4,128)S(1)} fusion(pred[4,128]{1,0:T(4,128)(4,1)S(1)} %iota_compare_fusion.2, bf16[512,128]{1,0:T(8,128)(2,1)S(1)} %get-tuple-element.93, bf16[16,512,128]{2,1,0:T(8,128)(2,1)} %get-tuple-element.92, s32[]{:T(128)S(6)} %copy.17), kind=kOutput, calls=%fused_computation.2.clone.1 | convolution fusion | flops 67631104 | bytes 270852 | tf_op jit(solution)/shard_map/while/body/eval_jaxpr/dot_general | solution.py:22
  36.3 0.1 reduce_sum.10
  36.5 1.2 %select_reduce_fusion.2 = f32[512,4]{0,1:T(4,128)S(1)} fusion(pred[4,128]{1,0:T(4,128)(4,1)S(1)} %iota_compare_fusion.2, bf16[512,128]{1,0:T(8,128)(2,1)S(1)} %get-tuple-element.93, bf16[16,512,128]{2,1,0:T(8,128)(2,1)} %get-tuple-element.92, s32[]{:T(128)S(6)} %copy.17), kind=kOutput, calls=%fused_computation.2.clone.1 | convolution fusion | flops 67631104 | bytes 270852 | tf_op jit(solution)/shard_map/while/body/eval_jaxpr/dot_general | solution.py:22
  37.8 0.1 reduce_sum.10
  38.0 1.2 %select_reduce_fusion.2 = f32[512,4]{0,1:T(4,128)S(1)} fusion(pred[4,128]{1,0:T(4,128)(4,1)S(1)} %iota_compare_fusion.2, bf16[512,128]{1,0:T(8,128)(2,1)S(1)} %get-tuple-element.93, bf16[16,512,128]{2,1,0:T(8,128)(2,1)} %get-tuple-element.92, s32[]{:T(128)S(6)} %copy.17), kind=kOutput, calls=%fused_computation.2.clone.1 | convolution fusion | flops 67631104 | bytes 270852 | tf_op jit(solution)/shard_map/while/body/eval_jaxpr/dot_general | solution.py:22
  39.3 0.1 reduce_sum.10
  39.5 1.2 %select_reduce_fusion.2 = f32[512,4]{0,1:T(4,128)S(1)} fusion(pred[4,128]{1,0:T(4,128)(4,1)S(1)} %iota_compare_fusion.2, bf16[512,128]{1,0:T(8,128)(2,1)S(1)} %get-tuple-element.93, bf16[16,512,128]{2,1,0:T(8,128)(2,1)} %get-tuple-element.92, s32[]{:T(128)S(6)} %copy.17), kind=kOutput, calls=%fused_computation.2.clone.1 | convolution fusion | flops 67631104 | bytes 270852 | tf_op jit(solution)/shard_map/while/body/eval_jaxpr/dot_general | solution.py:22
  40.8 0.1 reduce_sum.10
  40.9 0.1 reshape.91
  41.1 0.1 copy.11
  41.2 0.7 %reshape.92 = f32[4,1,256]{2,1,0:T(1,128)} reshape(f32[4,4,64]{2,1,0:T(4,128)S(1)} %copy.11) | data formatting | bytes 8192
  41.9 5.0 %all-to-all-start = ((f32[4,1,256]{2,1,0:T(1,128)}), f32[4,1,256]{2,1,0:T(1,128)S(1)}, u32[]{:S(2)}, u32[]{:S(2)}) async-start(f32[4,1,256]{2,1,0:T(1,128)} %reshape.92), calls=%async_computation | async-start | bytes 8192 | tf_op jit(solution)/shard_map/all_to_all | solution.py:36
  46.9 6.8 %gather_fusion = s32[1024]{0:T(1024)S(1)} fusion(s32[256]{0:T(256)S(1)} %copy-done, s32[1024]{0:T(1024)S(1)} %broadcast_clamp_fusion), kind=kCustom, calls=%fused_computation | custom fusion | bytes 12288 | tf_op jit(solution)/shard_map/jit(_take)/gather | solution.py:37
  53.8 0.5 broadcast.70
  54.3 0.7 %reduce = f32[4,256]{1,0:T(4,128)S(1)} reduce(f32[4,1,256]{2,1,0:T(1,128)S(1)} %all-to-all-done, f32[]{:T(128)} %broadcast.70), dimensions={1}, to_apply=%all_to_all.15.reduce_sub_computation | reduce | bytes 8196 | tf_op jit(solution)/shard_map/all_to_all | solution.py:36
  54.9 0.1 reshape.93
  55.0 0.1 all_to_all.17
  55.1 9.1 %gather_fusion.1 = f32[1024]{0:T(1024)S(1)} fusion(f32[4,256]{1,0:T(4,128)S(1)} %all_to_all.17, s32[1024]{0:T(1024)S(1)} %bitcast.43), kind=kCustom, calls=%fused_computation.1 | custom fusion | bytes 16384 | tf_op jit(solution)/shard_map/jit(take_along_axis)/gather | solution.py:37
  64.3 1.9 %sort_prefixfusion = f32[4,10]{1,0:T(4,128)} fusion(f32[4,256]{1,0:T(4,128)S(1)} %and_select_fusion), kind=kCustom, calls=%top_k.9.sort_prefix | custom fusion | flops 10240 | bytes 4256 | tf_op jit(solution)/shard_map/top_k | solution.py:38
  (79 shorter events, 2.7 us)
Async XLA Ops:
  0.6 46.2 %copy-start = (s32[256]{0:T(256)S(1)}, s32[256]{0:T(256)}, u32[]{:S(2)}) copy-start(s32[256]{0:T(256)} %param.10) | copy-start | bytes 3076
  0.6 46.2 %copy-start.1 = (s32[4,256]{1,0:T(4,128)S(1)}, s32[4,256]{1,0:T(4,128)}, u32[]{:S(2)}) copy-start(s32[4,256]{1,0:T(4,128)} %param.11) | copy-start | bytes 12292
  41.9 11.9 %all-to-all-start = ((f32[4,1,256]{2,1,0:T(1,128)}), f32[4,1,256]{2,1,0:T(1,128)S(1)}, u32[]{:S(2)}, u32[]{:S(2)}) async-start(f32[4,1,256]{2,1,0:T(1,128)} %reshape.92), calls=%async_computation | async-start | bytes 8192 | tf_op jit(solution)/shard_map/all_to_all | solution.py:36
  64.3 1.9 %copy-start.2 = (f32[4,256]{1,0:T(4,128)}, f32[4,256]{1,0:T(4,128)S(1)}, u32[]{:S(2)}) copy-start(f32[4,256]{1,0:T(4,128)S(1)} %and_select_fusion) | copy-start | bytes 12292
where the time goes:
time: 66.7 us; the launch traced here: 66.2 us
  local copies, waits for them, and re-layouts  19.8 us (30%)
  matrix products  19.6 us (29%)
  blocking collectives  15.3 us (23%)
  other arithmetic  5.42 us (8%)
  starting transfers between devices  4.96 us (7%)
  between operations  0.76 us (1%)
    dot_general x16, matrix products, one_block(): lax.dot_general(flat, piece, (((1,), (1,)), ((), ())), preferred_element_...  19.6 us
    all_gather x1, blocking collectives, shards(): lax.all_gather(queries, 'blk', axis=0, tiled=True)  15.3 us
    gather x2, local copies, waits for them, and re-layouts, shards(): jnp.take_along_axis(whole, jnp.take(slot_of, candidates, axis=0), axis=1)  9.13 us
    gather x2, local copies, waits for them, and re-layouts, shards(): jnp.take(slot_of, candidates, axis=0)  6.84 us
    all_to_all x1, starting transfers between devices, shards(): lax.all_to_all(table, 'blk', split_axis=0, concat_axis=1, tiled=True)  4.96 us
    top_k x1, other arithmetic, shards(): top = lax.top_k(score, TOPN)[0]  1.93 us
    reduce_sum x16, other arithmetic, one_block(): return jnp.sum(best.reshape(queries_here, tokens, group), axis=1) / tokens  1.43 us
  transfers between devices with their start and end apart: 1, of which 0 were waited for; matrix products, arithmetic and copies ran while one was open for 10% of the time, Pallas kernels for 0%

commit v1 on v0

v1 whole, which is shorter than its diff:
```python
import functools

import jax
import jax.numpy as jnp
from jax import lax
from jax.experimental import pallas as pl
from jax.experimental.pallas import tpu as pltpu
from jax.sharding import PartitionSpec as P

TOPN = 10
LANES = 128
ROWS = 8
MESH = pl.DeviceIdType.MESH


def lookup(tiles, width, index):
    tile_at, lane_at = index // width, index % width
    found = None
    for i, tile in enumerate(tiles):
        here = jnp.take_along_axis(tile, lane_at, axis=1, mode="promise_in_bounds")
        found = here if found is None else jnp.where(tile_at == i, here, found)
    return found


def kernel(n, lengths, slot_of, candidates, queries, passages, score_out, top_out,
           stored, asked, answer, replies, load_sem, query_sem, ask_send, ask_recv, reply_send, reply_recv):
    me = lax.axis_index("blk")
    count, span, width = passages.shape
    held, tokens, _ = queries.shape
    wide = held * tokens
    half = span // 2
    pieces = load_sem.shape[0]
    per_piece = count // pieces

    own_queries = pltpu.make_async_copy(queries, asked.at[0], query_sem)
    own_queries.start()
    loads = []
    for c in range(pieces):
        part = pl.ds(c * per_piece, per_piece)
        loads.append(pltpu.make_async_copy(passages.at[part], stored.at[part], load_sem.at[c]))
        loads[-1].start()

    barrier = pltpu.get_barrier_semaphore()
    for step in range(1, n):
        pl.semaphore_signal(barrier, inc=1, device_id={"blk": lax.rem(me + step, n)}, device_id_type=MESH)

    wanted = candidates[...]
    wanted = jnp.concatenate([wanted] * (ROWS // held), axis=0)
    ids = slot_of.shape[1]
    slots = [jnp.broadcast_to(slot_of[:, i:i + LANES], (ROWS, LANES)) for i in range(0, ids, LANES)]
    rows = [lookup(slots, LANES, wanted[:, i:i + LANES]) for i in range(0, wanted.shape[1], LANES)]

    own_queries.wait()
    pl.semaphore_wait(barrier, n - 1)
    asks = []
    for step in range(1, n):
        ask = pltpu.make_async_remote_copy(
            src_ref=asked.at[0], dst_ref=asked.at[step], send_sem=ask_send.at[step], recv_sem=ask_recv.at[step],
            device_id={"blk": lax.rem(me + step, n)}, device_id_type=MESH)
        ask.start()
        asks.append(ask)

    slot_at = lax.broadcasted_iota(jnp.int32, (span, width), 0)

    def fill(r, carry):
        piece = stored[r]
        first = jnp.broadcast_to(piece[0:1], (span, width))
        stored[r] = jnp.where(slot_at < lengths[r], piece, first)
        return carry

    for c in range(pieces):
        loads[c].wait()
        lax.fori_loop(c * per_piece, (c + 1) * per_piece, fill, 0, unroll=4)

    pick = lax.broadcasted_iota(jnp.int32, (ROWS, wide), 1) // tokens
    pick = jnp.where(pick == lax.broadcasted_iota(jnp.int32, (ROWS, wide), 0), 1.0 / tokens, 0.0).astype(jnp.bfloat16)
    group = 16

    def scores_of(source):
        flat = asked[source].reshape(wide, width)
        blank = jnp.zeros((wide, width), jnp.bfloat16)
        both = jnp.concatenate(
            [jnp.concatenate([flat, blank], axis=1), jnp.concatenate([blank, flat], axis=1)], axis=0)
        bests = []
        for g in range(0, count, group):
            piece = stored[g:g + group]
            pair = jnp.concatenate([piece[:, :half], piece[:, half:]], axis=2).reshape(group * half, 2 * width)
            similar = lax.dot_general(pair, both, (((1,), (1,)), ((), ())), preferred_element_type=jnp.float32)
            best = jnp.max(similar.reshape(group, half, 2 * wide), axis=1)
            bests.append(jnp.maximum(best[:, :wide], best[:, wide:]))
        best = jnp.concatenate(bests, axis=0)
        high = best.astype(jnp.bfloat16)
        low = (best - high.astype(jnp.float32)).astype(jnp.bfloat16)
        dims = (((1,), (1,)), ((), ()))
        return (lax.dot_general(pick, high, dims, preferred_element_type=jnp.float32)
                + lax.dot_general(pick, low, dims, preferred_element_type=jnp.float32))

    def put(ref, at, value):
        ref[at] = jnp.concatenate([value, jnp.zeros((ROWS, LANES - count), jnp.float32)], axis=1)

    put(replies, 0, scores_of(0))
    sends = []
    for step in range(1, n):
        asks[step - 1].wait_recv()
        put(answer, step, scores_of(step))
        back = pltpu.make_async_remote_copy(
            src_ref=answer.at[step], dst_ref=replies.at[step], send_sem=reply_send.at[step],
            recv_sem=reply_recv.at[step], device_id={"blk": lax.rem(me + n - step, n)}, device_id_type=MESH)
        back.start()
        sends.append(back)
    for send in sends:
        send.wait_recv()

    owners = [lax.rem(row // count + (n - me), n) * count + row % count for row in rows]
    tables = [replies[s] for s in range(n)]
    score = jnp.concatenate([lookup(tables, count, row) for row in owners], axis=1)
    score_out[...] = score[:held]

    total = score.shape[1]
    turned = jnp.transpose(score)
    earlier = lax.broadcasted_iota(jnp.int32, (total, total), 0) < lax.broadcasted_iota(jnp.int32, (total, total), 1)
    depth = top_out.shape[0]
    place = lax.broadcasted_iota(jnp.int32, (depth, total), 0).astype(jnp.float32)
    tops = jnp.zeros((depth, LANES), jnp.float32)
    lane = lax.broadcasted_iota(jnp.int32, (depth, LANES), 1)
    for q in range(held):
        here = score[q:q + 1]
        there = jnp.broadcast_to(turned[:, q:q + 1], (total, total))
        ahead = (there > here) | ((there == here) & earlier)
        rank = jnp.sum(jnp.where(ahead, 1.0, 0.0), axis=0, keepdims=True)
        chosen = jnp.sum(jnp.where(rank == place, here, 0.0), axis=1, keepdims=True)
        tops = jnp.where(lane == q, chosen, tops)
    top_out[...] = tops

    for copy in asks:
        copy.wait_send()
    for send in sends:
        send.wait_send()


def shards(n, queries, passages, lengths, slot_of, candidates):
    held, tokens, width = queries.shape
    depth = -(-TOPN // ROWS) * ROWS
    vmem = pl.BlockSpec(memory_space=pltpu.VMEM)
    hbm = pl.BlockSpec(memory_space=pl.ANY)
    score, top = pl.pallas_call(
        functools.partial(kernel, n),
        out_shape=(
            jax.ShapeDtypeStruct(candidates.shape, jnp.float32),
            jax.ShapeDtypeStruct((depth, LANES), jnp.float32),
        ),
        in_specs=[pl.BlockSpec(memory_space=pltpu.SMEM), vmem, vmem, hbm, hbm],
        out_specs=(vmem, vmem),
        scratch_shapes=[
            pltpu.VMEM(passages.shape, jnp.bfloat16),
            pltpu.VMEM((n, held, tokens, width), jnp.bfloat16),
            pltpu.VMEM((n, ROWS, LANES), jnp.float32),
            pltpu.VMEM((n, ROWS, LANES), jnp.float32),
            pltpu.SemaphoreType.DMA((4,)),
            pltpu.SemaphoreType.DMA,
            pltpu.SemaphoreType.DMA((n,)),
            pltpu.SemaphoreType.DMA((n,)),
            pltpu.SemaphoreType.DMA((n,)),
            pltpu.SemaphoreType.DMA((n,)),
        ],
        compiler_params=pltpu.CompilerParams(collective_id=0, has_side_effects=True),
    )(lengths, slot_of.reshape(1, -1), candidates, queries, passages)
    return score, jnp.transpose(top[:TOPN, :held])


def solution(mesh):
    return jax.shard_map(
        functools.partial(shards, mesh.shape["blk"]),
        mesh=mesh,
        in_specs=(
            P(("parts", "blk", "sub", "rep"), None, None),
            P(("parts", "blk"), None, None),
            P(("parts", "blk")),
            P("parts"),
            P(("parts", "blk", "sub", "rep"), None),
        ),
        out_specs=(
            P(("parts", "blk", "sub", "rep"), None),
            P(("parts", "blk", "sub", "rep"), None),
        ),
        check_vma=False,
    )
```

time: 66.7 us -> 20.7 us (0.31)
  matrix products: 19.6 us -> 0 us
  Pallas kernels: 0 us -> 17.2 us
  local copies, waits for them, and re-layouts: 19.8 us -> 2.63 us
  blocking collectives: 15.3 us -> 0 us
  other arithmetic: 5.42 us -> 0 us
  starting transfers between devices: 4.96 us -> 0 us
    dot_general x16 -> x0, matrix products: 19.6 us -> none  [one_block(): lax.dot_general(flat, piece, (((1,), (1,)), ((), ())), preferred_element_...]
    pallas_call x0 -> x1, Pallas kernels: none -> 17.2 us  [shards(): pl.pallas_call(functools.partial(kernel, n), out_shape=(jax.ShapeDtypeStr...]
    gather x4 -> x0, local copies, waits for them, and re-layouts: 16 us -> none  [the longest x2 9.13 us: shards(): jnp.take_along_axis(whole, jnp.take(slot_of, candidates, axis=0), axis=1)]
    all_gather x1 -> x0, blocking collectives: 15.3 us -> none  [shards(): lax.all_gather(queries, 'blk', axis=0, tiled=True)]
    all_to_all x1 -> x0, starting transfers between devices: 4.96 us -> none  [shards(): lax.all_to_all(table, 'blk', split_axis=0, concat_axis=1, tiled=True)]
    reshape x17 -> x0, local copies, waits for them, and re-layouts: 2.01 us -> none  [the longest x16 1.27 us: one_block(): return jnp.sum(best.reshape(queries_here, tokens, group), axis=1) / tokens]
    top_k x1 -> x0, other arithmetic: 1.93 us -> none  [shards(): top = lax.top_k(score, TOPN)[0]]
    reduce_sum x16 -> x0, other arithmetic: 1.43 us -> none  [one_block(): return jnp.sum(best.reshape(queries_here, tokens, group), axis=1) / tokens]
  transfers between devices with their start and end apart: 1 -> 0, of which waited for: 0 -> 0; matrix products, arithmetic and copies ran while one was open for 10% -> 0% of each run, Pallas kernels for 0% -> 0%
where the time goes in v1:
time: 20.7 us; the launch traced here: 20.4 us
  Pallas kernels  17.2 us (83%)
  local copies, waits for them, and re-layouts  2.63 us (13%)
  between operations  0.64 us (3%)
    pallas_call x1, Pallas kernels, shards(): pl.pallas_call(functools.partial(kernel, n), out_shape=(jax.ShapeDtypeStr...  17.2 us
    unnamed x2, local copies, waits for them, and re-layouts  1.93 us
    transpose x1, local copies, waits for them, and re-layouts, shards(): return (score, jnp.transpose(top[:TOPN, :held]))  0.7 us

profile of v1, /device:TPU:0, one launch (start us, length us, event | category | flops | bytes accessed | tf_op | source)
XLA Modules:
  0.0 20.4 jit_solution(7016045116288827825)
XLA Ops:
  0.6 17.2 %shard_map.68 = (f32[4,256]{1,0:T(4,128)}, f32[16,128]{1,0:T(8,128)}) custom-call(s32[64]{0:T(128)} %lengths.1, s32[1,256]{1,0:T(1,128)} %bitcast.3, s32[4,256]{1,0:T(4,128)} %candidates.1, bf16[4,32,128]{2,1,0:T(8,128)(2,1)} %queries.1, bf16[64,128,128]{2,1,0:T(8,128)(2,1)} %passages.1), custom_call_target="tpu_custom_call" | custom-call | tf_op jit(solution)/shard_map/pallas_call | solution.py:146
  17.8 0.7 %slice_bitcast_fusion = f32[4,10]{0,1:T(8,128)S(1)} fusion(f32[16,128]{1,0:T(8,128)} %get-tuple-element.5), kind=kLoop, calls=%fused_computation | loop fusion | bytes 320 | tf_op jit(solution)/shard_map/transpose | solution.py:168
  18.5 0.7 %copy.7 = f32[4,10]{1,0:T(4,128)} copy(f32[4,10]{0,1:T(8,128)S(1)} %slice_bitcast_fusion) | data formatting | bytes 320
  19.2 1.3 %copy.9 = f32[4,256]{1,0:T(4,128)} copy(f32[4,256]{1,0:T(4,128)} %get-tuple-element.10) | data formatting | bytes 8192

commit v2 on v1

v2 whole, which is shorter than its diff:
```python
import functools

import jax
import jax.numpy as jnp
from jax import lax
from jax.experimental import pallas as pl
from jax.experimental.pallas import tpu as pltpu
from jax.sharding import PartitionSpec as P

TOPN = 10
LANES = 128
ROWS = 8
MESH = pl.DeviceIdType.MESH


def split(index, width):
    if width & (width - 1):
        return lax.div(index, width), lax.rem(index, width)
    return lax.shift_right_logical(index, width.bit_length() - 1), index & (width - 1)


def lookup(tiles, places):
    tile_at, lane_at = places
    found = None
    for i, tile in enumerate(tiles):
        here = jnp.take_along_axis(tile, lane_at, axis=1, mode="promise_in_bounds")
        found = here if found is None else jnp.where(tile_at == i, here, found)
    return found


def peer_at(me, n, step):
    upper = lax.div(2 * me, n)
    room = me * (1 - upper) + (n - 1 - me) * upper
    inner = lax.div(step + 1, 2) * (1 - 2 * lax.rem(step + 1, 2))
    outer = (step - room) * (1 - 2 * upper)
    return me + jnp.where(step <= 2 * room, inner, outer)


def kernel(n, lengths_in, slot_in, wanted_in, queries, passages, score_out, top_out,
           stored, asked, answer, replies, lengths, slot_of, wanted_at,
           load_sem, small_sem, ask_send, ask_recv, reply_send, reply_recv):
    me = lax.axis_index("blk")
    count, span, width = passages.shape
    held, tokens, _ = queries.shape
    wide = held * tokens
    half = span // 2
    pieces = load_sem.shape[0]
    per_piece = count // pieces

    barrier = pltpu.get_barrier_semaphore()
    for step in range(1, n):
        pl.semaphore_signal(barrier, inc=1, device_id={"blk": lax.rem(me + step, n)}, device_id_type=MESH)

    smalls = []
    for i, (src, dst) in enumerate(((queries, asked.at[me]), (lengths_in, lengths), (slot_in, slot_of), (wanted_in, wanted_at))):
        smalls.append(pltpu.make_async_copy(src, dst, small_sem.at[i]))
        smalls[-1].start()
    loads = []
    for c in range(pieces):
        part = pl.ds(c * per_piece, per_piece)
        loads.append(pltpu.make_async_copy(passages.at[part], stored.at[part], load_sem.at[c]))
        loads[-1].start()

    def ask(step):
        peer = peer_at(me, n, step)
        return pltpu.make_async_remote_copy(
            src_ref=asked.at[me], dst_ref=asked.at[me], send_sem=ask_send.at[step], recv_sem=ask_recv.at[me],
            device_id={"blk": peer}, device_id_type=MESH)

    def asked_by(peer):
        return pltpu.make_async_remote_copy(
            src_ref=asked.at[me], dst_ref=asked.at[peer], send_sem=ask_send.at[0], recv_sem=ask_recv.at[peer],
            device_id={"blk": peer}, device_id_type=MESH)

    def reply(step):
        peer = peer_at(me, n, step)
        return pltpu.make_async_remote_copy(
            src_ref=answer.at[step], dst_ref=replies.at[me], send_sem=reply_send.at[step],
            recv_sem=reply_recv.at[me], device_id={"blk": peer}, device_id_type=MESH)

    def replied_by(peer):
        return pltpu.make_async_remote_copy(
            src_ref=answer.at[0], dst_ref=replies.at[peer], send_sem=reply_send.at[0],
            recv_sem=reply_recv.at[peer], device_id={"blk": peer}, device_id_type=MESH)

    smalls[0].wait()
    pl.semaphore_wait(barrier, n - 1)
    for step in range(1, n):
        ask(step).start()
    for small in smalls[1:]:
        small.wait()

    slot_at = lax.broadcasted_iota(jnp.int32, (span, width), 0)

    def fill(r, carry):
        piece = stored[r]
        first = jnp.broadcast_to(piece[0:1], (span, width))
        stored[r] = jnp.where(slot_at < lengths[r], piece, first)
        return carry

    for c in range(pieces):
        loads[c].wait()
        lax.fori_loop(c * per_piece, (c + 1) * per_piece, fill, 0, unroll=4)

    wanted = jnp.concatenate([wanted_at[...]] * (ROWS // held), axis=0)
    slots = [jnp.broadcast_to(slot_of[:, i:i + LANES], (ROWS, LANES)) for i in range(0, slot_of.shape[1], LANES)]
    rows = [lookup(slots, split(wanted[:, i:i + LANES], LANES)) for i in range(0, wanted.shape[1], LANES)]
    places = [split(row, count) for row in rows]

    pick = split(lax.broadcasted_iota(jnp.int32, (ROWS, wide), 1), tokens)[0]
    pick = jnp.where(pick == lax.broadcasted_iota(jnp.int32, (ROWS, wide), 0), 1.0 / tokens, 0.0).astype(jnp.bfloat16)
    group = 16

    def scores_of(source):
        flat = asked[source].reshape(wide, width)
        blank = jnp.zeros((wide, width), jnp.bfloat16)
        both = jnp.concatenate(
            [jnp.concatenate([flat, blank], axis=1), jnp.concatenate([blank, flat], axis=1)], axis=0)
        bests = []
        for g in range(0, count, group):
            piece = stored[g:g + group]
            pair = jnp.concatenate([piece[:, :half], piece[:, half:]], axis=2).reshape(group * half, 2 * width)
            similar = lax.dot_general(pair, both, (((1,), (1,)), ((), ())), preferred_element_type=jnp.float32)
            best = jnp.max(similar.reshape(group, half, 2 * wide), axis=1)
            bests.append(jnp.maximum(best[:, :wide], best[:, wide:]))
        best = jnp.concatenate(bests, axis=0)
        high = best.astype(jnp.bfloat16)
        low = (best - high.astype(jnp.float32)).astype(jnp.bfloat16)
        dims = (((1,), (1,)), ((), ()))
        table = (lax.dot_general(pick, high, dims, preferred_element_type=jnp.float32)
                 + lax.dot_general(pick, low, dims, preferred_element_type=jnp.float32))
        return jnp.concatenate([table, jnp.zeros((ROWS, LANES - count), jnp.float32)], axis=1)

    replies[me] = scores_of(me)

    def serve(step, carry):
        peer = peer_at(me, n, step)
        asked_by(peer).wait_recv()
        answer[step] = scores_of(peer)
        reply(step).start()
        return carry

    lax.fori_loop(1, n, serve, 0)

    for step in range(1, n):
        replied_by(peer_at(me, n, step)).wait_recv()

    tables = [replies[s] for s in range(n)]
    score = jnp.concatenate([lookup(tables, place) for place in places], axis=1)
    score_out[...] = score[:held]

    total = score.shape[1]
    turned = jnp.transpose(score)
    earlier = lax.broadcasted_iota(jnp.int32, (total, total), 0) < lax.broadcasted_iota(jnp.int32, (total, total), 1)
    depth = -(-TOPN // ROWS) * ROWS
    place = lax.broadcasted_iota(jnp.int32, (depth, total), 0).astype(jnp.float32)
    tops = jnp.zeros((depth, LANES), jnp.float32)
    lane = lax.broadcasted_iota(jnp.int32, (depth, LANES), 1)
    for q in range(held):
        here = score[q:q + 1]
        there = jnp.broadcast_to(turned[:, q:q + 1], (total, total))
        ahead = (there > here) | ((there == here) & earlier)
        rank = jnp.sum(jnp.where(ahead, 1.0, 0.0), axis=0, keepdims=True)
        chosen = jnp.sum(jnp.where(rank == place, here, 0.0), axis=1, keepdims=True)
        tops = jnp.where(lane == q, chosen, tops)
    top_out[...] = jnp.transpose(tops)[:held, :TOPN]

    for step in range(1, n):
        ask(step).wait_send()
        reply(step).wait_send()


def publish(score_in, top_in, score_out, top_out):
    score_out[...] = score_in[...]
    top_out[...] = top_in[...]


def shards(n, queries, passages, lengths, slot_of, candidates):
    held, tokens, width = queries.shape
    vmem = pl.BlockSpec(memory_space=pltpu.VMEM)
    hbm = pl.BlockSpec(memory_space=pl.ANY)
    slot_row = slot_of.reshape(1, -1)
    results = [(candidates.shape, jnp.float32), ((held, TOPN), jnp.float32)]
    score, top = pl.pallas_call(
        functools.partial(kernel, n),
        out_shape=tuple(pltpu.VMEM(shape, dtype) for shape, dtype in results),
        in_specs=[hbm] * 5,
        out_specs=(vmem, vmem),
        scratch_shapes=[
            pltpu.VMEM(passages.shape, jnp.bfloat16),
            pltpu.VMEM((n, held, tokens, width), jnp.bfloat16),
            pltpu.VMEM((n, ROWS, LANES), jnp.float32),
            pltpu.VMEM((n, ROWS, LANES), jnp.float32),
            pltpu.SMEM(lengths.shape, jnp.int32),
            pltpu.VMEM(slot_row.shape, jnp.int32),
            pltpu.VMEM(candidates.shape, jnp.int32),
            pltpu.SemaphoreType.DMA((4,)),
            pltpu.SemaphoreType.DMA((4,)),
            pltpu.SemaphoreType.DMA((n,)),
            pltpu.SemaphoreType.DMA((n,)),
            pltpu.SemaphoreType.DMA((n,)),
            pltpu.SemaphoreType.DMA((n,)),
        ],
        compiler_params=pltpu.CompilerParams(collective_id=0, has_side_effects=True),
    )(lengths, slot_row, candidates, queries, passages)
    return pl.pallas_call(
        publish,
        out_shape=tuple(jax.ShapeDtypeStruct(shape, dtype) for shape, dtype in results),
        in_specs=[vmem, vmem],
        compiler_params=pltpu.CompilerParams(vmem_limit_bytes=1 << 20),
        out_specs=(vmem, vmem),
    )(score, top)


def solution(mesh):
    return jax.shard_map(
        functools.partial(shards, mesh.shape["blk"]),
        mesh=mesh,
        in_specs=(
            P(("parts", "blk", "sub", "rep"), None, None),
            P(("parts", "blk"), None, None),
            P(("parts", "blk")),
            P("parts"),
            P(("parts", "blk", "sub", "rep"), None),
        ),
        out_specs=(
            P(("parts", "blk", "sub", "rep"), None),
            P(("parts", "blk", "sub", "rep"), None),
        ),
        check_vma=False,
    )
```

time: 20.7 us -> 17.3 us (0.84)
  local copies, waits for them, and re-layouts: 2.63 us -> 0 us
  Pallas kernels: 17.2 us -> 16.5 us
    unnamed x2 -> x0, local copies, waits for them, and re-layouts: 1.93 us -> none
    transpose x1 -> x0, local copies, waits for them, and re-layouts: 0.7 us -> none  [shards(): return (score, jnp.transpose(top[:TOPN, :held]))]
    pallas_call x1 -> x2, Pallas kernels: 17.2 us -> 16.5 us  [the longest x1 15.9 us: shards(): pl.pallas_call(functools.partial(kernel, n), out_shape=tuple((pltpu.VMEM(...]
where the time goes in v2:
time: 17.3 us; the launch traced here: 17.2 us
  Pallas kernels  16.5 us (95%)
  between operations  0.64 us (4%)
    pallas_call x1, Pallas kernels, shards(): pl.pallas_call(functools.partial(kernel, n), out_shape=tuple((pltpu.VMEM(...  15.9 us
    pallas_call x1, Pallas kernels, shards(): pl.pallas_call(publish, out_shape=tuple((jax.ShapeDtypeStruct(shape, dtyp...  0.6 us

profile of v2, /device:TPU:0, one launch (start us, length us, event | category | flops | bytes accessed | tf_op | source)
XLA Modules:
  0.0 17.2 jit_solution(4862531781776474472)
XLA Ops:
  0.6 15.9 %shard_map.68 = (f32[4,256]{1,0:T(4,128)S(1)}, f32[4,10]{1,0:T(4,128)S(1)}) custom-call(s32[64]{0:T(128)} %lengths_in.1, s32[1,256]{1,0:T(1,128)} %bitcast.1, s32[4,256]{1,0:T(4,128)} %wanted_in.1, bf16[4,32,128]{2,1,0:T(8,128)(2,1)} %queries.1, bf16[64,128,128]{2,1,0:T(8,128)(2,1)} %passages.1), custom_call_target="tpu_custom_call" | custom-call | tf_op jit(solution)/shard_map/pallas_call | solution.py:184
  16.6 0.6 %shard_map.69 = (f32[4,256]{1,0:T(4,128)}, f32[4,10]{1,0:T(4,128)}) custom-call(f32[4,256]{1,0:T(4,128)S(1)} %get-tuple-element.4.score_in, f32[4,10]{1,0:T(4,128)S(1)} %get-tuple-element.5.top_in), custom_call_target="tpu_custom_call" | custom-call | tf_op jit(solution)/shard_map/pallas_call | solution.py:206

commit v3 on v2

--- a/solution.py
+++ b/solution.py
@@ -36,10 +36,16 @@
     return me + jnp.where(step <= 2 * room, inner, outer)
 
 
-def kernel(n, lengths_in, slot_in, wanted_in, queries, passages, score_out, top_out,
+def source_at(me, n, step):
+    at = n - step
+    return at - jnp.where(at <= me, 1, 0)
+
+
+def kernel(n, copies, lengths_in, slot_in, wanted_in, queries, passages, score_out, top_out,
            stored, asked, answer, replies, lengths, slot_of, wanted_at,
            load_sem, small_sem, ask_send, ask_recv, reply_send, reply_recv):
     me = lax.axis_index("blk")
+    other = copies - 1 - lax.axis_index("rep")
     count, span, width = passages.shape
     held, tokens, _ = queries.shape
     wide = held * tokens
@@ -49,7 +55,7 @@
 
     barrier = pltpu.get_barrier_semaphore()
     for step in range(1, n):
-        pl.semaphore_signal(barrier, inc=1, device_id={"blk": lax.rem(me + step, n)}, device_id_type=MESH)
+        pl.semaphore_signal(barrier, inc=1, device_id={"blk": lax.rem(me + step, n), "rep": other}, device_id_type=MESH)
 
     smalls = []
     for i, (src, dst) in enumerate(((queries, asked.at[me]), (lengths_in, lengths), (slot_in, slot_of), (wanted_in, wanted_at))):
@@ -65,27 +71,27 @@
         peer = peer_at(me, n, step)
         return pltpu.make_async_remote_copy(
             src_ref=asked.at[me], dst_ref=asked.at[me], send_sem=ask_send.at[step], recv_sem=ask_recv.at[me],
-            device_id={"blk": peer}, device_id_type=MESH)
+            device_id={"blk": peer, "rep": other}, device_id_type=MESH)
 
     def asked_by(peer):
         return pltpu.make_async_remote_copy(
             src_ref=asked.at[me], dst_ref=asked.at[peer], send_sem=ask_send.at[0], recv_sem=ask_recv.at[peer],
-            device_id={"blk": peer}, device_id_type=MESH)
+            device_id={"blk": peer, "rep": other}, device_id_type=MESH)
 
     def reply(step):
-        peer = peer_at(me, n, step)
+        peer = source_at(me, n, step)
         return pltpu.make_async_remote_copy(
             src_ref=answer.at[step], dst_ref=replies.at[me], send_sem=reply_send.at[step],
-            recv_sem=reply_recv.at[me], device_id={"blk": peer}, device_id_type=MESH)
+            recv_sem=reply_recv.at[me], device_id={"blk": peer, "rep": other}, device_id_type=MESH)
 
     def replied_by(peer):
         return pltpu.make_async_remote_copy(
             src_ref=answer.at[0], dst_ref=replies.at[peer], send_sem=reply_send.at[0],
-            recv_sem=reply_recv.at[peer], device_id={"blk": peer}, device_id_type=MESH)
+            recv_sem=reply_recv.at[peer], device_id={"blk": peer, "rep": other}, device_id_type=MESH)
 
     smalls[0].wait()
     pl.semaphore_wait(barrier, n - 1)
-    for step in range(1, n):
+    for step in range(n - 1, 0, -1):
         ask(step).start()
     for small in smalls[1:]:
         small.wait()
@@ -134,7 +140,7 @@
     replies[me] = scores_of(me)
 
     def serve(step, carry):
-        peer = peer_at(me, n, step)
+        peer = source_at(me, n, step)
         asked_by(peer).wait_recv()
         answer[step] = scores_of(peer)
         reply(step).start()
@@ -175,14 +181,14 @@
     top_out[...] = top_in[...]
 
 
-def shards(n, queries, passages, lengths, slot_of, candidates):
+def shards(n, copies, queries, passages, lengths, slot_of, candidates):
     held, tokens, width = queries.shape
     vmem = pl.BlockSpec(memory_space=pltpu.VMEM)
     hbm = pl.BlockSpec(memory_space=pl.ANY)
     slot_row = slot_of.reshape(1, -1)
     results = [(candidates.shape, jnp.float32), ((held, TOPN), jnp.float32)]
     score, top = pl.pallas_call(
-        functools.partial(kernel, n),
+        functools.partial(kernel, n, copies),
         out_shape=tuple(pltpu.VMEM(shape, dtype) for shape, dtype in results),
         in_specs=[hbm] * 5,
         out_specs=(vmem, vmem),
@@ -214,7 +220,7 @@
 
 def solution(mesh):
     return jax.shard_map(
-        functools.partial(shards, mesh.shape["blk"]),
+        functools.partial(shards, mesh.shape["blk"], mesh.shape["rep"]),
         mesh=mesh,
         in_specs=(
             P(("parts", "blk", "sub", "rep"), None, None),

time: 17.3 us -> 15.9 us (0.919)
  Pallas kernels: 16.5 us -> 15.1 us
    pallas_call x1, Pallas kernels: 15.9 us -> 14.5 us  [shards(): pl.pallas_call(functools.partial(kernel, n, copies), out_shape=tuple((plt...]
where the time goes in v3:
time: 15.9 us; the launch traced here: 15.8 us
  Pallas kernels  15.1 us (95%)
  between operations  0.64 us (4%)
    pallas_call x1, Pallas kernels, shards(): pl.pallas_call(functools.partial(kernel, n, copies), out_shape=tuple((plt...  14.5 us
    pallas_call x1, Pallas kernels, shards(): pl.pallas_call(publish, out_shape=tuple((jax.ShapeDtypeStruct(shape, dtyp...  0.6 us

profile of v3, /device:TPU:0, one launch (start us, length us, event | category | flops | bytes accessed | tf_op | source)
XLA Modules:
  0.0 15.8 jit_solution(8425963584643894425)
XLA Ops:
  0.6 14.5 %shard_map.68 = (f32[4,256]{1,0:T(4,128)S(1)}, f32[4,10]{1,0:T(4,128)S(1)}) custom-call(s32[64]{0:T(128)} %lengths_in.1, s32[1,256]{1,0:T(1,128)} %bitcast.1, s32[4,256]{1,0:T(4,128)} %wanted_in.1, bf16[4,32,128]{2,1,0:T(8,128)(2,1)} %queries.1, bf16[64,128,128]{2,1,0:T(8,128)(2,1)} %passages.1), custom_call_target="tpu_custom_call" | custom-call | tf_op jit(solution)/shard_map/pallas_call | solution.py:190
  15.2 0.6 %shard_map.69 = (f32[4,256]{1,0:T(4,128)}, f32[4,10]{1,0:T(4,128)}) custom-call(f32[4,256]{1,0:T(4,128)S(1)} %get-tuple-element.4.score_in, f32[4,10]{1,0:T(4,128)S(1)} %get-tuple-element.5.top_in), custom_call_target="tpu_custom_call" | custom-call | tf_op jit(solution)/shard_map/pallas_call | solution.py:212

commit v4 on v3

--- a/solution.py
+++ b/solution.py
@@ -148,16 +148,21 @@
 
     lax.fori_loop(1, n, serve, 0)
 
+    def from_owner(owner, score):
+        table = replies[owner]
+        return [jnp.where(tile_at == owner, jnp.take_along_axis(table, lane_at, axis=1, mode="promise_in_bounds"), found)
+                for (tile_at, lane_at), found in zip(places, score)]
+
+    score = from_owner(me, [jnp.zeros((ROWS, LANES), jnp.float32)] * len(places))
     for step in range(1, n):
-        replied_by(peer_at(me, n, step)).wait_recv()
-
-    tables = [replies[s] for s in range(n)]
-    score = jnp.concatenate([lookup(tables, place) for place in places], axis=1)
+        owner = peer_at(me, n, step)
+        replied_by(owner).wait_recv()
+        score = from_owner(owner, score)
+    score = jnp.concatenate(score, axis=1)
     score_out[...] = score[:held]
 
     total = score.shape[1]
     turned = jnp.transpose(score)
-    earlier = lax.broadcasted_iota(jnp.int32, (total, total), 0) < lax.broadcasted_iota(jnp.int32, (total, total), 1)
     depth = -(-TOPN // ROWS) * ROWS
     place = lax.broadcasted_iota(jnp.int32, (depth, total), 0).astype(jnp.float32)
     tops = jnp.zeros((depth, LANES), jnp.float32)
@@ -165,9 +170,8 @@
     for q in range(held):
         here = score[q:q + 1]
         there = jnp.broadcast_to(turned[:, q:q + 1], (total, total))
-        ahead = (there > here) | ((there == here) & earlier)
-        rank = jnp.sum(jnp.where(ahead, 1.0, 0.0), axis=0, keepdims=True)
-        chosen = jnp.sum(jnp.where(rank == place, here, 0.0), axis=1, keepdims=True)
+        larger = jnp.sum(jnp.where(there > here, 1.0, 0.0), axis=0, keepdims=True)
+        chosen = jnp.min(jnp.where(larger <= place, here, jnp.inf), axis=1, keepdims=True)
         tops = jnp.where(lane == q, chosen, tops)
     top_out[...] = jnp.transpose(tops)[:held, :TOPN]
 

time: 15.9 us -> 16 us (level)
  no operation moved by 1% of the time
where the time goes in v4:
time: 16 us; the launch traced here: 15.8 us
  Pallas kernels  15.2 us (95%)
  between operations  0.64 us (4%)
    pallas_call x1, Pallas kernels, shards(): pl.pallas_call(functools.partial(kernel, n, copies), out_shape=tuple((plt...  14.6 us
    pallas_call x1, Pallas kernels, shards(): pl.pallas_call(publish, out_shape=tuple((jax.ShapeDtypeStruct(shape, dtyp...  0.6 us

profile of v4, /device:TPU:0, one launch (start us, length us, event | category | flops | bytes accessed | tf_op | source)
XLA Modules:
  0.0 15.8 jit_solution(17390009287954690486)
XLA Ops:
  0.6 14.6 %shard_map.68 = (f32[4,256]{1,0:T(4,128)S(1)}, f32[4,10]{1,0:T(4,128)S(1)}) custom-call(s32[64]{0:T(128)} %lengths_in.1, s32[1,256]{1,0:T(1,128)} %bitcast.1, s32[4,256]{1,0:T(4,128)} %wanted_in.1, bf16[4,32,128]{2,1,0:T(8,128)(2,1)} %queries.1, bf16[64,128,128]{2,1,0:T(8,128)(2,1)} %passages.1), custom_call_target="tpu_custom_call" | custom-call | tf_op jit(solution)/shard_map/pallas_call | solution.py:194
  15.2 0.6 %shard_map.69 = (f32[4,256]{1,0:T(4,128)}, f32[4,10]{1,0:T(4,128)}) custom-call(f32[4,256]{1,0:T(4,128)S(1)} %get-tuple-element.4.score_in, f32[4,10]{1,0:T(4,128)S(1)} %get-tuple-element.5.top_in), custom_call_target="tpu_custom_call" | custom-call | tf_op jit(solution)/shard_map/pallas_call | solution.py:216

commit v5 on v4

--- a/solution.py
+++ b/solution.py
@@ -37,8 +37,8 @@
 
 
 def source_at(me, n, step):
-    at = n - step
-    return at - jnp.where(at <= me, 1, 0)
+    at = step - 1
+    return at + jnp.where(at >= me, 1, 0)
 
 
 def kernel(n, copies, lengths_in, slot_in, wanted_in, queries, passages, score_out, top_out,

time: 16 us -> 14.7 us (0.919)
  Pallas kernels: 15.2 us -> 13.9 us
    pallas_call x1, Pallas kernels: 14.6 us -> 13.3 us  [shards(): pl.pallas_call(functools.partial(kernel, n, copies), out_shape=tuple((plt...]
where the time goes in v5:
time: 14.7 us; the launch traced here: 14.6 us
  Pallas kernels  13.9 us (95%)
  between operations  0.64 us (4%)
    pallas_call x1, Pallas kernels, shards(): pl.pallas_call(functools.partial(kernel, n, copies), out_shape=tuple((plt...  13.3 us
    pallas_call x1, Pallas kernels, shards(): pl.pallas_call(publish, out_shape=tuple((jax.ShapeDtypeStruct(shape, dtyp...  0.6 us

profile of v5, /device:TPU:0, one launch (start us, length us, event | category | flops | bytes accessed | tf_op | source)
XLA Modules:
  0.0 14.6 jit_solution(13817961517181262987)
XLA Ops:
  0.6 13.3 %shard_map.68 = (f32[4,256]{1,0:T(4,128)S(1)}, f32[4,10]{1,0:T(4,128)S(1)}) custom-call(s32[64]{0:T(128)} %lengths_in.1, s32[1,256]{1,0:T(1,128)} %bitcast.1, s32[4,256]{1,0:T(4,128)} %wanted_in.1, bf16[4,32,128]{2,1,0:T(8,128)(2,1)} %queries.1, bf16[64,128,128]{2,1,0:T(8,128)(2,1)} %passages.1), custom_call_target="tpu_custom_call" | custom-call | tf_op jit(solution)/shard_map/pallas_call | solution.py:194
  14.0 0.6 %shard_map.69 = (f32[4,256]{1,0:T(4,128)}, f32[4,10]{1,0:T(4,128)}) custom-call(f32[4,256]{1,0:T(4,128)S(1)} %get-tuple-element.4.score_in, f32[4,10]{1,0:T(4,128)S(1)} %get-tuple-element.5.top_in), custom_call_target="tpu_custom_call" | custom-call | tf_op jit(solution)/shard_map/pallas_call | solution.py:216

commit v6 on v5

--- a/solution.py
+++ b/solution.py
@@ -115,7 +115,8 @@
 
     pick = split(lax.broadcasted_iota(jnp.int32, (ROWS, wide), 1), tokens)[0]
     pick = jnp.where(pick == lax.broadcasted_iota(jnp.int32, (ROWS, wide), 0), 1.0 / tokens, 0.0).astype(jnp.bfloat16)
-    group = 16
+    pick = jnp.concatenate([pick, pick], axis=1)
+    group = 4
 
     def scores_of(source):
         flat = asked[source].reshape(wide, width)
@@ -132,9 +133,8 @@
         best = jnp.concatenate(bests, axis=0)
         high = best.astype(jnp.bfloat16)
         low = (best - high.astype(jnp.float32)).astype(jnp.bfloat16)
-        dims = (((1,), (1,)), ((), ()))
-        table = (lax.dot_general(pick, high, dims, preferred_element_type=jnp.float32)
-                 + lax.dot_general(pick, low, dims, preferred_element_type=jnp.float32))
+        halves = jnp.concatenate([high, low], axis=1)
+        table = lax.dot_general(pick, halves, (((1,), (1,)), ((), ())), preferred_element_type=jnp.float32)
         return jnp.concatenate([table, jnp.zeros((ROWS, LANES - count), jnp.float32)], axis=1)
 
     replies[me] = scores_of(me)
@@ -169,8 +169,11 @@
     lane = lax.broadcasted_iota(jnp.int32, (depth, LANES), 1)
     for q in range(held):
         here = score[q:q + 1]
-        there = jnp.broadcast_to(turned[:, q:q + 1], (total, total))
-        larger = jnp.sum(jnp.where(there > here, 1.0, 0.0), axis=0, keepdims=True)
+        larger = jnp.zeros((ROWS, total), jnp.float32)
+        for k in range(0, total, ROWS):
+            there = jnp.broadcast_to(turned[k:k + ROWS, q:q + 1], (ROWS, total))
+            larger = jnp.where(there > here, larger + 1.0, larger)
+        larger = jnp.sum(larger, axis=0, keepdims=True)
         chosen = jnp.min(jnp.where(larger <= place, here, jnp.inf), axis=1, keepdims=True)
         tops = jnp.where(lane == q, chosen, tops)
     top_out[...] = jnp.transpose(tops)[:held, :TOPN]

time: 14.7 us -> 14.7 us (level)
  no operation moved by 1% of the time
where the time goes in v6:
time: 14.7 us; the launch traced here: 14.5 us
  Pallas kernels  13.9 us (95%)
  between operations  0.64 us (4%)
    pallas_call x1, Pallas kernels, shards(): pl.pallas_call(functools.partial(kernel, n, copies), out_shape=tuple((plt...  13.3 us
    pallas_call x1, Pallas kernels, shards(): pl.pallas_call(publish, out_shape=tuple((jax.ShapeDtypeStruct(shape, dtyp...  0.6 us

profile of v6, /device:TPU:0, one launch (start us, length us, event | category | flops | bytes accessed | tf_op | source)
XLA Modules:
  0.0 14.5 jit_solution(2707583113545025797)
XLA Ops:
  0.6 13.3 %shard_map.68 = (f32[4,256]{1,0:T(4,128)S(1)}, f32[4,10]{1,0:T(4,128)S(1)}) custom-call(s32[64]{0:T(128)} %lengths_in.1, s32[1,256]{1,0:T(1,128)} %bitcast.1, s32[4,256]{1,0:T(4,128)} %wanted_in.1, bf16[4,32,128]{2,1,0:T(8,128)(2,1)} %queries.1, bf16[64,128,128]{2,1,0:T(8,128)(2,1)} %passages.1), custom_call_target="tpu_custom_call" | custom-call | tf_op jit(solution)/shard_map/pallas_call | solution.py:197
  13.9 0.6 %shard_map.69 = (f32[4,256]{1,0:T(4,128)}, f32[4,10]{1,0:T(4,128)}) custom-call(f32[4,256]{1,0:T(4,128)S(1)} %get-tuple-element.4.score_in, f32[4,10]{1,0:T(4,128)S(1)} %get-tuple-element.5.top_in), custom_call_target="tpu_custom_call" | custom-call | tf_op jit(solution)/shard_map/pallas_call | solution.py:219

commit v7 on v6

--- a/solution.py
+++ b/solution.py
@@ -68,7 +68,7 @@
         loads[-1].start()
 
     def ask(step):
-        peer = peer_at(me, n, step)
+        peer = source_at(me, n, step)
         return pltpu.make_async_remote_copy(
             src_ref=asked.at[me], dst_ref=asked.at[me], send_sem=ask_send.at[step], recv_sem=ask_recv.at[me],
             device_id={"blk": peer, "rep": other}, device_id_type=MESH)

time: 14.7 us -> 14.7 us (level)
  no operation moved by 1% of the time
where the time goes in v7:
time: 14.7 us; the launch traced here: 14.5 us
  Pallas kernels  13.9 us (95%)
  between operations  0.64 us (4%)
    pallas_call x1, Pallas kernels, shards(): pl.pallas_call(functools.partial(kernel, n, copies), out_shape=tuple((plt...  13.3 us
    pallas_call x1, Pallas kernels, shards(): pl.pallas_call(publish, out_shape=tuple((jax.ShapeDtypeStruct(shape, dtyp...  0.6 us

profile of v7, /device:TPU:0, one launch (start us, length us, event | category | flops | bytes accessed | tf_op | source)
XLA Modules:
  0.0 14.5 jit_solution(9966124548041299813)
XLA Ops:
  0.6 13.3 %shard_map.68 = (f32[4,256]{1,0:T(4,128)S(1)}, f32[4,10]{1,0:T(4,128)S(1)}) custom-call(s32[64]{0:T(128)} %lengths_in.1, s32[1,256]{1,0:T(1,128)} %bitcast.1, s32[4,256]{1,0:T(4,128)} %wanted_in.1, bf16[4,32,128]{2,1,0:T(8,128)(2,1)} %queries.1, bf16[64,128,128]{2,1,0:T(8,128)(2,1)} %passages.1), custom_call_target="tpu_custom_call" | custom-call | tf_op jit(solution)/shard_map/pallas_call | solution.py:197
  13.9 0.6 %shard_map.69 = (f32[4,256]{1,0:T(4,128)}, f32[4,10]{1,0:T(4,128)}) custom-call(f32[4,256]{1,0:T(4,128)S(1)} %get-tuple-element.4.score_in, f32[4,10]{1,0:T(4,128)S(1)} %get-tuple-element.5.top_in), custom_call_target="tpu_custom_call" | custom-call | tf_op jit(solution)/shard_map/pallas_call | solution.py:219
